TPU v7x, 32 devices: a whole 2x2x4 slice. The times are simulated.
32 devices in a mesh: band: 2 (over core), tmpl: 8 (over z, x), tm: 2 (over y).
Axes of the slice: x: 2, y: 2, z: 4, core: 2. Of those that a mesh axis runs over, the one named last changes fastest.
Arguments:
- strain_high: float32 [16384], P('tm'), may hold values from -6 to 6
- strain_mid: float32 [2048], P('tm'), may hold values from -6 to 6
- strain_low: float32 [256], P('tm'), may hold values from -6 to 6
- filters_high: float32 [320, 1024], P('tmpl'), may hold values from -0.1875 to 0.1875
- filters_mid: float32 [320, 1024], P('tmpl'), may hold values from -0.1875 to 0.1875
- filters_low: float32 [320, 128], P('tmpl'), may hold values from -0.5 to 0.5
- recon_high: float32 [320, 2, 2048], P(None, None, 'tmpl'), may hold values from -0.3125 to 0.3125
- recon_mid: float32 [320, 2, 2048], P(None, None, 'tmpl'), may hold values from -0.3125 to 0.3125
- recon_low: float32 [320, 2, 2048], P(None, None, 'tmpl'), may hold values from -0.3125 to 0.3125
- basis_count: int32 [3], replicated, may hold values from 160 to 320
Outputs:
- snr: float32 [2, 2048, 16384], P('band', 'tmpl', 'tm')
Inputs may be any that keep to these rules, and one draw needn't show every extreme that they name: basis_count[b] says how many of the first 320 basis vectors band b uses.
All inputs are finite; a program needn't handle non-finite values.
Results may differ from a plain program's by a relative error of at most 0.000082.
Values sent between devices are 32-bit elements; how exact they have to be, the bound alone decides.
A program may use at most 128 MiB of HBM per device.

v0:
```python
import functools
import math

import jax
import jax.numpy as jnp
import numpy as np
from jax import lax
from jax.experimental import pallas as pl
from jax.experimental.pallas import tpu as pltpu
from jax.sharding import PartitionSpec as P

RATIO = 8
HALF_TAPS = 8
LANES = 128
WIDE = 256
MESH = pl.DeviceIdType.MESH


def upsample_matrix(rows, cols):
    u = np.arange(rows)[:, None]
    v = np.arange(cols)[None, :]
    lag = u - v // RATIO
    offset = (v % RATIO) / RATIO - (lag - HALF_TAPS)
    value = np.sinc(offset) * (0.5 + 0.5 * np.cos(np.pi * offset / (HALF_TAPS + 1)))
    return np.where((lag >= 0) & (lag < 2 * HALF_TAPS), value, 0.0).astype(np.float32)


def gather_kernel(
    sizes, low_ref, mid_ref, high_ref, strain_ref,
    low_all, mid_all, high_all, strain_all,
    send_sem, recv_sem, fsend_sem, frecv_sem, ssend_sem, srecv_sem,
):
    bands, peers, slices = sizes
    b, p, y = lax.axis_index("band"), lax.axis_index("tmpl"), lax.axis_index("tm")
    barrier = pltpu.get_barrier_semaphore()
    others = [(b, lax.rem(p + k, peers), y) for k in range(1, peers)]
    others += [(b, p, lax.rem(y + k, slices)) for k in range(1, slices)]
    others += [(1 - b, p, y)]
    for device in others:
        pl.semaphore_signal(barrier, inc=1, device_id=device, device_id_type=MESH)
    pl.semaphore_wait(barrier, len(others))

    strain_sends = []
    for k in range(1, slices):
        copy = pltpu.make_async_remote_copy(
            src_ref=strain_ref, dst_ref=strain_all.at[y],
            send_sem=ssend_sem.at[k], recv_sem=srecv_sem.at[k],
            device_id=(b, p, lax.rem(y + k, slices)), device_id_type=MESH,
        )
        copy.start()
        strain_sends.append(copy)

    mid_half = mid_ref.shape[1] // 2
    high_half = high_ref.shape[1] // 2
    mid_cols = pl.ds(pl.multiple_of(b * mid_half, LANES), mid_half)
    high_cols = pl.ds(pl.multiple_of(b * high_half, LANES), high_half)
    sends = {}
    for k in range(1, peers):
        target = (b, lax.rem(p + k, peers), y)
        pairs = (
            (low_ref, low_all.at[p]),
            (mid_ref.at[:, mid_cols], mid_all.at[p, :, mid_cols]),
            (high_ref.at[:, high_cols], high_all.at[p, :, high_cols]),
        )
        for a, (src, dst) in enumerate(pairs):
            copy = pltpu.make_async_remote_copy(
                src_ref=src, dst_ref=dst,
                send_sem=send_sem.at[a, k], recv_sem=recv_sem.at[a, k],
                device_id=target, device_id_type=MESH,
            )
            copy.start()
            sends[a, k] = copy
    low_all[p] = low_ref[...]
    mid_all[p] = mid_ref[...]
    high_all[p] = high_ref[...]
    strain_all[y] = strain_ref[...]

    forwards = []
    for k in range(1, peers):
        source = lax.rem(p + peers - k, peers)
        sends[0, k].wait_recv()
        for a, ref, cols in ((1, mid_all, mid_cols), (2, high_all, high_cols)):
            sends[a, k].wait_recv()
            view = ref.at[source, :, cols]
            copy = pltpu.make_async_remote_copy(
                src_ref=view, dst_ref=view,
                send_sem=fsend_sem.at[a - 1, k], recv_sem=frecv_sem.at[a - 1, k],
                device_id=(1 - b, p, y), device_id_type=MESH,
            )
            copy.start()
            forwards.append(copy)
    for copy in sends.values():
        copy.wait_send()
    for copy in strain_sends + forwards:
        copy.wait()


def gather(sizes, low, mid, high, strain):
    bands, peers, slices = sizes
    vmem = pl.BlockSpec(memory_space=pltpu.VMEM)
    shapes = [jax.ShapeDtypeStruct((peers,) + a.shape, a.dtype) for a in (low, mid, high)]
    shapes += [jax.ShapeDtypeStruct((slices,) + strain.shape, strain.dtype)]
    dma = pltpu.SemaphoreType.DMA
    return pl.pallas_call(
        functools.partial(gather_kernel, sizes),
        out_shape=shapes,
        in_specs=[vmem] * 4,
        out_specs=[vmem] * 4,
        scratch_shapes=[
            dma((3, peers)), dma((3, peers)), dma((2, peers)), dma((2, peers)),
            dma((slices,)), dma((slices,)),
        ],
        compiler_params=pltpu.CompilerParams(collective_id=0, has_side_effects=True),
        name="gather_filters",
    )(low, mid, high, strain)


def split(value):
    top = value.astype(jnp.bfloat16)
    return top, (value - top.astype(jnp.float32)).astype(jnp.bfloat16)


def dot3(a, b, dims=(((1,), (0,)), ((), ()))):
    def one(u, v):
        return lax.dot_general(u, v, dims, preferred_element_type=jnp.float32)

    return one(a[0], b[0]) + one(a[0], b[1]) + one(a[1], b[0])


def rolled(x_ref, row):
    base = jnp.broadcast_to(x_ref[pl.ds(row, 1), :], (LANES, LANES))
    return pltpu.roll(base, 0, 1, stride=1, stride_axis=0)


def fill_frames(x_ref, top_ref, rest_ref, chunks):
    lane = lax.broadcasted_iota(jnp.int32, (LANES, LANES), 1)
    lag = lax.broadcasted_iota(jnp.int32, (LANES, LANES), 0)

    def step(c, before):
        now = rolled(x_ref, c + 1)
        top, rest = split(jnp.where(lane >= lag, now, before))
        left = pl.multiple_of((chunks - 1 - c) * LANES, LANES)
        right = pl.multiple_of((chunks - c) * LANES, LANES)
        for ref, value in ((top_ref, top), (rest_ref, rest)):
            ref[pl.ds(left, LANES), :LANES] = value
            ref[pl.ds(right, LANES), LANES:] = value
        return now

    lax.fori_loop(0, chunks, step, rolled(x_ref, 0))


def compute_kernel(
    dims, clock_ref, low_f, mid_f, high_f, low_r, mid_r, high_r, x_low, x_mid, x_high, g_ref,
    out_ref,
    fl_top, fl_rest, fm_top, fm_rest, fh_top, fh_rest, w_top, w_rest, wm_top, wm_rest,
    p_top, p_rest, g_top, g_rest,
):
    low_here, mid_here, low_total, mid_total = dims
    step = pl.program_id(0)
    y = clock_ref[0]
    taps = high_f.shape[1]
    taps_mid = mid_f.shape[1]
    width = out_ref.shape[2]
    first = (((0,), (0,)), ((), ()))

    @pl.when(step == 0)
    def _():
        top, rest = split(g_ref[...])
        g_top[...] = top
        g_rest[...] = rest
        fill_frames(x_low, fl_top, fl_rest, x_low.shape[0] - 1)
        fill_frames(x_mid, fm_top, fm_rest, x_mid.shape[0] - 1)
        fill_frames(x_high, fh_top, fh_rest, x_high.shape[0] - 1)
        rows = lax.broadcasted_iota(jnp.int32, low_r.shape, 0)
        low_w = dot3(split(jnp.where(rows < clock_ref[3], low_r[...], 0.0)), split(low_f[...]), first)
        mid_w = dot3(split(jnp.where(rows < clock_ref[2], mid_r[...], 0.0)), split(mid_f[...]), first)
        high_w = dot3(split(jnp.where(rows < clock_ref[1], high_r[...], 0.0)), split(high_f[...]), first)
        wm_top[...], wm_rest[...] = split(mid_w)
        w_top[...], w_rest[...] = split(high_w)
        low_w = split(low_w)
        low_chunks = x_low.shape[0] - 1
        parts = []
        for c in range(low_chunks):
            at = (low_chunks - 1 - c) * LANES
            frames = (fl_top[at : at + LANES, :LANES], fl_rest[at : at + LANES, :LANES])
            parts.append(dot3(low_w, frames))
        low = jnp.concatenate(parts, axis=1)
        time = y * low_here - (HALF_TAPS + 1) + lax.broadcasted_iota(jnp.int32, low.shape, 1)
        low = split(jnp.where((time >= 0) & (time < low_total), low, 0.0))
        mid_chunks = x_mid.shape[0] - 1
        cols = p_top.shape[1]
        for start in range(0, cols, WIDE):
            size = min(WIDE, cols - start)
            at = (mid_chunks - taps_mid // LANES - start // LANES) * LANES
            frames = (fm_top[at : at + taps_mid, :size], fm_rest[at : at + taps_mid, :size])
            value = dot3((wm_top[...], wm_rest[...]), frames)
            base, lead = start // g_ref.shape[1] * LANES, start % g_ref.shape[1]
            pieces = tuple(v[:, base : base + WIDE] for v in low)
            value += dot3(pieces, (g_top[:, lead : lead + size], g_rest[:, lead : lead + size]))
            time = y * mid_here - HALF_TAPS + start + lax.broadcasted_iota(jnp.int32, value.shape, 1)
            top, rest = split(jnp.where((time >= 0) & (time < mid_total), value, 0.0))
            p_top[:, start : start + size] = top
            p_rest[:, start : start + size] = rest

    high_chunks = x_high.shape[0] - 1
    base = pl.multiple_of(step * (width // RATIO), LANES)
    pieces = (p_top[:, pl.ds(base, WIDE)], p_rest[:, pl.ds(base, WIDE)])
    for start in range(0, width, WIDE):
        at = (high_chunks - taps // LANES - start // LANES - step * (width // LANES)) * LANES
        rows = pl.ds(pl.multiple_of(at, LANES), taps)
        value = dot3((w_top[...], w_rest[...]), (fh_top[rows, :], fh_rest[rows, :]))
        tile = slice(start, start + WIDE)
        out_ref[0, :, tile] = value + dot3(pieces, (g_top[:, tile], g_rest[:, tile]))


def compute(dims, clock, filters, recons, strains):
    low_here, mid_here, low_total, mid_total = dims
    tmpl = recons[0].shape[1]
    x_low, x_mid, x_high = strains
    taps = filters[2].shape[1]
    samples = x_high.shape[0] * LANES - taps
    width = RATIO * LANES
    cols = mid_here + LANES
    g = jnp.asarray(upsample_matrix(WIDE, width))
    half = jnp.bfloat16

    def frames(x):
        return [pltpu.VMEM((x.shape[0] * LANES, WIDE), half)] * 2

    full = [pl.BlockSpec(memory_space=pltpu.VMEM)] * 10
    return pl.pallas_call(
        functools.partial(compute_kernel, dims),
        grid=(samples // width,),
        out_shape=jax.ShapeDtypeStruct((1, tmpl, samples), jnp.float32),
        in_specs=[pl.BlockSpec(memory_space=pltpu.SMEM)] + full,
        out_specs=pl.BlockSpec((1, tmpl, width), lambda i: (0, 0, i)),
        scratch_shapes=frames(x_low) + frames(x_mid) + frames(x_high)
        + [pltpu.VMEM((tmpl, taps), half)] * 2
        + [pltpu.VMEM((tmpl, filters[1].shape[1]), half)] * 2
        + [pltpu.VMEM((tmpl, cols), half)] * 2
        + [pltpu.VMEM((WIDE, width), half)] * 2,
        compiler_params=pltpu.CompilerParams(vmem_limit_bytes=60 * 1024 * 1024),
        name="filter_templates",
    )(clock, *filters, *recons, x_low, x_mid, x_high, g)


def local(
    sizes, strain_high, strain_mid, strain_low, filters_high, filters_mid, filters_low,
    recon_high, recon_mid, recon_low, basis_count,
):
    bands, peers, slices = sizes
    b, y = lax.axis_index("band"), lax.axis_index("tm")
    n_high, n_mid, n_low = strain_high.shape[0], strain_mid.shape[0], strain_low.shape[0]
    packed = jnp.concatenate([strain_high, strain_mid, strain_low]).reshape(-1, LANES)
    low, mid, high, strains = gather(sizes, filters_low, filters_mid, filters_high, packed)
    strains = strains.reshape(slices, -1)

    def window(start, count, before, rows):
        whole = strains[:, start : start + count].reshape(-1)
        whole = jnp.pad(whole, (before, rows * LANES))
        return lax.dynamic_slice(whole, (y * count,), (rows * LANES,)).reshape(rows, LANES)

    taps_high, taps_mid, taps_low = (f.shape[1] for f in (filters_high, filters_mid, filters_low))
    x_high = window(0, n_high, taps_high, (n_high + taps_high) // LANES)
    x_mid = window(n_high, n_mid, taps_mid + HALF_TAPS, (n_mid + LANES + taps_mid) // LANES)
    x_low = window(n_high + n_mid, n_low, taps_low + HALF_TAPS + 1, (n_low + 2 * LANES + taps_low) // LANES)

    def part(recon):
        return lax.dynamic_index_in_dim(recon, b, 1, keepdims=False)

    def flat(f):
        return f.reshape(-1, f.shape[2])

    clock = jnp.concatenate([y[None].astype(jnp.int32), basis_count])
    return compute(
        (n_low, n_mid, n_low * slices, n_mid * slices), clock,
        (flat(low), flat(mid), flat(high)),
        (part(recon_low), part(recon_mid), part(recon_high)),
        (x_low, x_mid, x_high),
    )


def solution(mesh):
    sizes = tuple(mesh.shape[name] for name in ("band", "tmpl", "tm"))
    in_specs = (
        P("tm"), P("tm"), P("tm"),
        P("tmpl", None), P("tmpl", None), P("tmpl", None),
        P(None, None, "tmpl"), P(None, None, "tmpl"), P(None, None, "tmpl"),
        P(),
    )
    return jax.shard_map(
        functools.partial(local, sizes), mesh=mesh, in_specs=in_specs,
        out_specs=P("band", "tmpl", "tm"), check_vma=False,
    )
```

profile of v0, /device:TPU:27, one launch (start us, length us, event | category | flops | bytes accessed | tf_op | source)
XLA Modules:
  0.0 85.1 jit_solution(8059660902627022479)
XLA Ops:
  0.0 0.0 copy-start
  0.0 0.0 copy-start.2
  0.0 0.0 copy-start.1
  0.0 1.4 %pad_add_fusion.clock_ref = s32[4]{0:T(128)} fusion(s32[3]{0:T(128)} %param.20, s32[1]{0:T(128)} %bitcast), kind=kLoop, calls=%fused_computation.18 | loop fusion | flops 4 | bytes 32 | tf_op jit(solution)/shard_map/concatenate | solution.py:274
  1.4 1.4 %maximum_bitcast_fusion.strain_ref = f32[73,128]{1,0:T(8,128)} fusion(f32[128]{0:T(128)} %param.13, f32[1024]{0:T(1024)} %param.12, f32[8192]{0:T(1024)} %param.11), kind=kLoop, calls=%fused_computation.6 | loop fusion | flops 18688 | bytes 74752 | tf_op jit(solution)/shard_map/reshape | solution.py:254
  2.8 0.0 copy-done
  2.8 0.3 constant_dynamic-slice_fusion.2
  3.1 0.7 copy.28
  3.9 0.0 copy-done.2
  3.9 0.0 copy-done.1
  3.9 0.7 constant_dynamic-slice_fusion
  4.6 0.7 copy.26
  5.3 0.8 copy.27
  6.1 41.0 %gather_filters.1 = (f32[8,40,128]{2,1,0:T(8,128)}, f32[8,40,1024]{2,1,0:T(8,128)}, f32[8,40,1024]{2,1,0:T(8,128)}, f32[2,73,128]{2,1,0:T(8,128)}) custom-call(f32[40,128]{1,0:T(8,128)} %low_ref.1, f32[40,1024]{1,0:T(8,128)} %mid_ref.1, f32[40,1024]{1,0:T(8,128)} %high_ref.1, f32[73,128]{1,0:T(8,128)} %maximum_bitcast_fusion.strain_ref), custom_call_target="tpu_custom_call" | custom-call | tf_op jit(solution)/shard_map/gather_filters/pallas_call | solution.py:104
  47.1 0.9 %copy.29 = f32[1,2,73,128]{3,1,2,0:T(2,128)S(1)} copy(f32[1,2,73,128]{3,2,1,0:T(8,128)} %bitcast.45) | data formatting | bytes 149504
  48.1 0.7 fusion.2.x_low
  48.8 0.6 fusion.x_high
  49.4 0.7 fusion.1.x_mid
  50.1 35.0 %filter_templates.1 = f32[1,256,8192]{2,1,0:T(8,128)} custom-call(s32[4]{0:T(128)} %pad_add_fusion.clock_ref, f32[320,128]{1,0:T(8,128)} %bitcast.44, f32[320,1024]{1,0:T(8,128)} %bitcast.38, f32[320,1024]{1,0:T(8,128)} %bitcast.39, f32[320,256]{1,0:T(8,128)} %bitcast.35, f32[320,256]{1,0:T(8,128)} %bitcast.37, f32[320,256]{1,0:T(8,128)} %bitcast.36, ...), custom_call_target="tpu_custom_call" | custom-call | tf_op jit(solution)/shard_map/filter_templates/pallas_call | solution.py:231
  (5 shorter events, 0.0 us)
Async XLA Ops:
  0.0 2.8 %copy-start = (f32[320,2,256]{2,1,0:T(2,128)S(1)}, f32[320,2,256]{2,1,0:T(2,128)}, u32[]{:S(2)}) copy-start(f32[320,2,256]{2,1,0:T(2,128)} %param.19) | copy-start | bytes 1966084
  0.0 3.9 %copy-start.2 = (f32[320,2,256]{2,1,0:T(2,128)S(1)}, f32[320,2,256]{2,1,0:T(2,128)}, u32[]{:S(2)}) copy-start(f32[320,2,256]{2,1,0:T(2,128)} %param.18) | copy-start | bytes 1966084
  0.0 3.9 %copy-start.1 = (f32[320,2,256]{2,1,0:T(2,128)S(1)}, f32[320,2,256]{2,1,0:T(2,128)}, u32[]{:S(2)}) copy-start(f32[320,2,256]{2,1,0:T(2,128)} %param.17) | copy-start | bytes 1966084
where the time goes:
time: 85.3 us; the launch traced here: 85.1 us
  Pallas kernels  76.1 us (89%)
  local copies, waits for them, and re-layouts  6.16 us (7%)
  other arithmetic  2.81 us (3%)
    pallas_call x1, Pallas kernels, gather(): pl.pallas_call(functools.partial(gather_kernel, sizes), out_shape=shapes,...  41 us
    pallas_call x1, Pallas kernels, compute(): pl.pallas_call(functools.partial(compute_kernel, dims), grid=(samples //...  35 us
    unnamed x14, local copies, waits for them, and re-layouts  3.22 us
    reshape x3, local copies, waits for them, and re-layouts, window(): lax.dynamic_slice(whole, (y * count,), (rows * LANES,)).reshape(rows, LANES)  1.98 us

commit v1 on v0

v1 whole, which is shorter than its diff:
```python
import functools
import math

import jax
import jax.numpy as jnp
import numpy as np
from jax import lax
from jax.experimental import pallas as pl
from jax.experimental.pallas import tpu as pltpu
from jax.sharding import PartitionSpec as P

RATIO = 8
HALF_TAPS = 8
LANES = 128
WIDE = 256
MESH = pl.DeviceIdType.MESH


def upsample_matrix(rows, cols):
    u = np.arange(rows)[:, None]
    v = np.arange(cols)[None, :]
    lag = u - v // RATIO
    offset = (v % RATIO) / RATIO - (lag - HALF_TAPS)
    value = np.sinc(offset) * (0.5 + 0.5 * np.cos(np.pi * offset / (HALF_TAPS + 1)))
    return np.where((lag >= 0) & (lag < 2 * HALF_TAPS), value, 0.0).astype(np.float32)


def gather_kernel(
    sizes, low_ref, mid_ref, high_ref, sl_ref, sm_ref, sh_ref,
    low_all, mid_all, high_all, sl_all, sm_all, sh_prev,
    strain_send, strain_recv, lz_send, lz_recv, lx_send, lx_recv,
    z_send, z_recv, x_send, x_recv, y_send, y_recv, d_send, d_recv, c_send, c_recv,
):
    bands, peers, slices, lines, parts = sizes
    rings = peers // lines
    b, p, y = lax.axis_index("band"), lax.axis_index("tmpl"), lax.axis_index("tm")
    z, x = p // lines, p % lines
    part = y % parts

    def along_z(k):
        return (b, ((z + k) % rings) * lines + x, y)

    def along_y(m):
        return (b, p, y - part + (part + m) % parts)

    across = (b, z * lines + (x + 1) % lines, y)
    sibling = (1 - b, p, y)
    barrier = pltpu.get_barrier_semaphore()
    others = [along_z(k) for k in range(1, rings)] + [sibling]
    others += [(b, p, (y + k) % slices) for k in range(1, slices)]
    if lines > 1:
        others += [across]
    for device in others:
        pl.semaphore_signal(barrier, inc=1, device_id=device, device_id_type=MESH)
    pl.semaphore_wait(barrier, len(others))

    sent, landed = [], []

    def send(src, dst, sems, at, device):
        copy = pltpu.make_async_remote_copy(
            src_ref=src, dst_ref=dst, send_sem=sems[0].at[at], recv_sem=sems[1].at[at],
            device_id=device, device_id_type=MESH,
        )
        copy.start()
        sent.append(copy)
        return copy

    strain = (strain_send, strain_recv)
    for k in range(1, slices):
        device = (b, p, (y + k) % slices)
        landed.append(send(sl_ref, sl_all.at[2 + y], strain, (0, k), device))
        landed.append(send(sm_ref, sm_all.at[2 + y], strain, (1, k), device))
    if slices > 1:
        tail = sh_prev.shape[0]
        last = sh_ref.at[pl.ds(sh_ref.shape[0] - tail, tail)]
        landed.append(send(last, sh_prev, strain, (2, 1), (b, p, (y + 1) % slices)))

    arrays = ((mid_ref, mid_all), (high_ref, high_all))
    size = [ref.shape[1] // (bands * parts) for ref, _ in arrays]

    def cols(a, m=0):
        start = (b * parts + (part + m) % parts) * size[a]
        return pl.ds(pl.multiple_of(start, LANES), size[a])

    def shard(k, other=0):
        return ((z + rings - k) % rings) * lines + (x + other) % lines

    low_z = {k: send(low_ref, low_all.at[p], (lz_send, lz_recv), k, along_z(k)) for k in range(1, rings)}
    from_z, from_x, from_y, from_d = {}, {}, {}, {}
    low_x = {}
    if lines > 1:
        low_x[0] = send(low_ref, low_all.at[p], (lx_send, lx_recv), 0, across)
    for a, (ref, full) in enumerate(arrays):
        for k in range(1, rings):
            from_z[a, k] = send(
                ref.at[:, cols(a)], full.at[p, :, cols(a)], (z_send, z_recv), (a, k), along_z(k)
            )
        if lines > 1:
            for m in range(parts):
                piece = send(
                    ref.at[:, cols(a, m)], full.at[p, :, cols(a, m)],
                    (x_send, x_recv) if m == 0 else (d_send, d_recv), (a, m, 0), across,
                )
                (from_x if m == 0 else from_d)[a, m, 0] = piece
    low_all[p] = low_ref[...]
    mid_all[p] = mid_ref[...]
    high_all[p] = high_ref[...]
    for ref, value in ((sl_all, sl_ref), (sm_all, sm_ref)):
        zero = jnp.zeros(value.shape, jnp.float32)
        ref[0] = zero
        ref[1] = zero
        ref[slices + 2] = zero
        ref[slices + 3] = zero
        ref[2 + y] = value[...]
    if slices == 1:
        sh_prev[...] = jnp.zeros(sh_prev.shape, jnp.float32)

    count = [0]

    def pass_on(a, view):
        at = (a, count[0])
        count[0] += 1
        landed.append(send(view, view, (c_send, c_recv), at, sibling))

    for k in range(1, rings):
        low_z[k].wait_recv()
        if lines > 1:
            view = low_all.at[shard(k)]
            low_x[k] = send(view, view, (lx_send, lx_recv), k, across)
    for a, (_, full) in enumerate(arrays):
        count[0] = 0
        for k in range(1, rings):
            from_z[a, k].wait_recv()
            view = full.at[shard(k), :, cols(a)]
            if lines > 1:
                from_x[a, 0, k] = send(view, view, (x_send, x_recv), (a, 0, k), across)
            for m in range(1, parts):
                from_y[a, m, k] = send(view, view, (y_send, y_recv), (a, m, k), along_y(m))
            pass_on(a, view)
    base = count[0]
    for a, (_, full) in enumerate(arrays):
        count[0] = base
        for k in range(rings):
            if lines > 1:
                from_x[a, 0, k].wait_recv()
                view = full.at[shard(k, 1), :, cols(a)]
                if k % 2 == 1:
                    for m in range(1, parts):
                        from_d[a, m, k] = send(view, view, (d_send, d_recv), (a, m, k), along_y(m))
                pass_on(a, view)
            for m in range(1, parts):
                if k == 0:
                    continue
                from_y[a, m, k].wait_recv()
                view = full.at[shard(k), :, cols(a, parts - m)]
                if lines > 1 and k % 2 == 0:
                    from_d[a, m, k] = send(view, view, (d_send, d_recv), (a, m, k), across)
                pass_on(a, view)
    base = count[0]
    for a, (_, full) in enumerate(arrays):
        count[0] = base
        for k in range(rings):
            for m in range(1, parts):
                if lines > 1:
                    from_d[a, m, k].wait_recv()
                    shift = m if k == 0 else parts - m
                    pass_on(a, full.at[shard(k, 1), :, cols(a, shift)])
    for copy in low_x.values():
        copy.wait_recv()
    for copy in landed:
        copy.wait_recv()
    for copy in sent:
        copy.wait_send()


def gather(sizes, low, mid, high, s_low, s_mid, s_high):
    bands, peers, slices = sizes
    lines = 2 if peers % 2 == 0 else 1
    rings = peers // lines
    parts = math.gcd(slices, min(mid.shape[1], high.shape[1]) // (bands * LANES))
    vmem = pl.BlockSpec(memory_space=pltpu.VMEM)
    f32 = jnp.float32
    shapes = [jax.ShapeDtypeStruct((peers,) + a.shape, f32) for a in (low, mid, high)]
    shapes += [jax.ShapeDtypeStruct((slices + 4,) + a.shape, f32) for a in (s_low, s_mid)]
    shapes += [jax.ShapeDtypeStruct((high.shape[1] // LANES, LANES), f32)]
    dma = pltpu.SemaphoreType.DMA
    two = lambda *dims: [dma(dims)] * 2
    return pl.pallas_call(
        functools.partial(gather_kernel, (bands, peers, slices, lines, parts)),
        out_shape=shapes,
        in_specs=[vmem] * 6,
        out_specs=[vmem] * 6,
        scratch_shapes=two(3, slices) + two(rings) + two(rings) + two(2, rings)
        + two(2, parts, rings) * 3 + two(2, peers * parts),
        compiler_params=pltpu.CompilerParams(collective_id=0, has_side_effects=True),
        name="gather_filters",
    )(low, mid, high, s_low, s_mid, s_high)


def split(value):
    top = value.astype(jnp.bfloat16)
    return top, (value - top.astype(jnp.float32)).astype(jnp.bfloat16)


def dot3(a, b, dims=(((1,), (0,)), ((), ()))):
    def one(u, v):
        return lax.dot_general(u, v, dims, preferred_element_type=jnp.float32)

    return one(a[0], b[0]) + one(a[0], b[1]) + one(a[1], b[0])


def staggered(row):
    return pltpu.roll(jnp.broadcast_to(row, (LANES, LANES)), 0, 1, stride=1, stride_axis=0)


def shifted(read, by):
    lane = lax.broadcasted_iota(jnp.int32, (1, LANES), 1)

    def row(r):
        late = [pltpu.roll(read(r + i), by, 1) for i in range(2)]
        return jnp.where(lane >= by, late[1], late[0])

    return row


def fill_frames(row, top_ref, rest_ref, chunks):
    lane = lax.broadcasted_iota(jnp.int32, (LANES, LANES), 1)
    lag = lax.broadcasted_iota(jnp.int32, (LANES, LANES), 0)

    def step(c, before):
        now = staggered(row(c + 1))
        top, rest = split(jnp.where(lane >= lag, now, before))
        left = pl.multiple_of((chunks - 1 - c) * LANES, LANES)
        right = pl.multiple_of((chunks - c) * LANES, LANES)
        for ref, value in ((top_ref, top), (rest_ref, rest)):
            ref[pl.ds(left, LANES), :LANES] = value
            ref[pl.ds(right, LANES), LANES:] = value
        return now

    lax.fori_loop(0, chunks, step, staggered(row(0)))


def compute_kernel(
    dims, count_ref, low_f, mid_f, high_f, x_low, x_mid, x_prev, x_high, g_ref,
    recon_low, recon_mid, recon_high,
    out_ref, low_r, mid_r, high_r, recon_sem, x_full,
    fl_top, fl_rest, fm_top, fm_rest, fh_top, fh_rest, w_top, w_rest, wm_top, wm_rest,
    p_top, p_rest, g_top, g_rest,
):
    low_here, mid_here, low_total, mid_total = dims
    step = pl.program_id(0)
    y = lax.axis_index("tm")
    taps = high_f.shape[1]
    taps_mid = mid_f.shape[1]
    taps_low = low_f.shape[1]
    low_chunks, mid_chunks, high_chunks = (r.shape[0] // LANES - 1 for r in (fl_top, fm_top, fh_top))
    width = out_ref.shape[2]
    first = (((0,), (0,)), ((), ()))

    @pl.when(step == 0)
    def _():
        top, rest = split(g_ref[...])
        g_top[...] = top
        g_rest[...] = rest
        band = lax.axis_index("band")
        copies = []
        for i, (src, dst) in enumerate(((recon_low, low_r), (recon_mid, mid_r), (recon_high, high_r))):
            copy = pltpu.make_async_copy(src.at[:, band, :], dst, recon_sem.at[i])
            copy.start()
            copies.append(copy)
        before = x_prev.shape[0]
        x_full[:before] = jnp.where(y > 0, x_prev[...], 0.0)
        x_full[before:] = x_high[...]
        low_first = y + 2 - taps_low // LANES - 1
        mid_first = (y + 2) * (mid_here // LANES) - taps_mid // LANES - 1
        low_row = shifted(lambda r: x_low[low_first + r], HALF_TAPS + 1)
        mid_row = shifted(lambda r: x_mid[pl.ds(mid_first + r, 1), :], HALF_TAPS)
        fill_frames(low_row, fl_top, fl_rest, low_chunks)
        fill_frames(mid_row, fm_top, fm_rest, mid_chunks)
        fill_frames(lambda r: x_full[pl.ds(r, 1), :], fh_top, fh_rest, high_chunks)
        for copy in copies:
            copy.wait()
        rows = lax.broadcasted_iota(jnp.int32, low_r.shape, 0)
        low_w = dot3(split(jnp.where(rows < count_ref[2], low_r[...], 0.0)), split(low_f[...]), first)
        mid_w = dot3(split(jnp.where(rows < count_ref[1], mid_r[...], 0.0)), split(mid_f[...]), first)
        high_w = dot3(split(jnp.where(rows < count_ref[0], high_r[...], 0.0)), split(high_f[...]), first)
        wm_top[...], wm_rest[...] = split(mid_w)
        w_top[...], w_rest[...] = split(high_w)
        low_w = split(low_w)
        parts = []
        for c in range(low_chunks):
            at = (low_chunks - 1 - c) * LANES
            frames = (fl_top[at : at + LANES, :LANES], fl_rest[at : at + LANES, :LANES])
            parts.append(dot3(low_w, frames))
        low = jnp.concatenate(parts, axis=1)
        time = y * low_here - (HALF_TAPS + 1) + lax.broadcasted_iota(jnp.int32, low.shape, 1)
        low = split(jnp.where((time >= 0) & (time < low_total), low, 0.0))
        cols = p_top.shape[1]
        for start in range(0, cols, WIDE):
            size = min(WIDE, cols - start)
            at = (mid_chunks - taps_mid // LANES - start // LANES) * LANES
            frames = (fm_top[at : at + taps_mid, :size], fm_rest[at : at + taps_mid, :size])
            value = dot3((wm_top[...], wm_rest[...]), frames)
            base, lead = start // g_ref.shape[1] * LANES, start % g_ref.shape[1]
            pieces = tuple(v[:, base : base + WIDE] for v in low)
            value += dot3(pieces, (g_top[:, lead : lead + size], g_rest[:, lead : lead + size]))
            time = y * mid_here - HALF_TAPS + start + lax.broadcasted_iota(jnp.int32, value.shape, 1)
            top, rest = split(jnp.where((time >= 0) & (time < mid_total), value, 0.0))
            p_top[:, start : start + size] = top
            p_rest[:, start : start + size] = rest

    base = pl.multiple_of(step * (width // RATIO), LANES)
    pieces = (p_top[:, pl.ds(base, WIDE)], p_rest[:, pl.ds(base, WIDE)])
    for start in range(0, width, WIDE):
        at = (high_chunks - taps // LANES - start // LANES - step * (width // LANES)) * LANES
        rows = pl.ds(pl.multiple_of(at, LANES), taps)
        value = dot3((w_top[...], w_rest[...]), (fh_top[rows, :], fh_rest[rows, :]))
        tile = slice(start, start + WIDE)
        out_ref[0, :, tile] = value + dot3(pieces, (g_top[:, tile], g_rest[:, tile]))


def compute(dims, count, filters, recons, strains):
    low_here, mid_here, low_total, mid_total = dims
    basis, _, tmpl = recons[0].shape
    taps_low, taps_mid, taps = (f.shape[1] for f in filters)
    samples = strains[3].shape[0] * LANES
    width = RATIO * LANES
    cols = mid_here + LANES
    g = jnp.asarray(upsample_matrix(WIDE, width))
    half = jnp.bfloat16

    def frames(rows):
        return [pltpu.VMEM((rows, WIDE), half)] * 2

    return pl.pallas_call(
        functools.partial(compute_kernel, dims),
        grid=(samples // width,),
        out_shape=jax.ShapeDtypeStruct((1, tmpl, samples), jnp.float32),
        in_specs=[pl.BlockSpec(memory_space=pltpu.SMEM)]
        + [pl.BlockSpec(memory_space=pltpu.VMEM)] * 8
        + [pl.BlockSpec(memory_space=pl.ANY)] * 3,
        out_specs=pl.BlockSpec((1, tmpl, width), lambda i: (0, 0, i)),
        scratch_shapes=[pltpu.VMEM((basis, tmpl), jnp.float32)] * 3
        + [pltpu.SemaphoreType.DMA((3,)), pltpu.VMEM(((samples + taps) // LANES, LANES), jnp.float32)]
        + frames(low_here + 2 * LANES + taps_low) + frames(cols + taps_mid) + frames(samples + taps)
        + [pltpu.VMEM((tmpl, taps), half)] * 2
        + [pltpu.VMEM((tmpl, taps_mid), half)] * 2
        + [pltpu.VMEM((tmpl, cols), half)] * 2
        + [pltpu.VMEM((WIDE, width), half)] * 2,
        compiler_params=pltpu.CompilerParams(vmem_limit_bytes=60 * 1024 * 1024),
        name="filter_templates",
    )(count, *filters, *strains, g, *recons)


def local(
    sizes, strain_high, strain_mid, strain_low, filters_high, filters_mid, filters_low,
    recon_high, recon_mid, recon_low, basis_count,
):
    slices = sizes[2]
    n_mid, n_low = strain_mid.shape[0], strain_low.shape[0]
    s_low, s_mid, s_high = (s.reshape(-1, LANES) for s in (strain_low, strain_mid, strain_high))
    low, mid, high, x_low, x_mid, x_prev = gather(
        sizes, filters_low, filters_mid, filters_high, s_low, s_mid, s_high
    )

    def flat(f):
        return f.reshape(-1, f.shape[2])

    return compute(
        (n_low, n_mid, n_low * slices, n_mid * slices), basis_count,
        (flat(low), flat(mid), flat(high)),
        (recon_low, recon_mid, recon_high),
        (x_low, flat(x_mid), x_prev, s_high),
    )


def solution(mesh):
    sizes = tuple(mesh.shape[name] for name in ("band", "tmpl", "tm"))
    in_specs = (
        P("tm"), P("tm"), P("tm"),
        P("tmpl", None), P("tmpl", None), P("tmpl", None),
        P(None, None, "tmpl"), P(None, None, "tmpl"), P(None, None, "tmpl"),
        P(),
    )
    return jax.shard_map(
        functools.partial(local, sizes), mesh=mesh, in_specs=in_specs,
        out_specs=P("band", "tmpl", "tm"), check_vma=False,
    )
```

time: 85.3 us -> 65 us (0.76)
  the two profiles are of different devices: /device:TPU:27 before, /device:TPU:1 now
where the time goes in v1:
time: 65 us; the launch traced here: 64.9 us
  Pallas kernels  64.8 us (100%)
    pallas_call x1, Pallas kernels, compute(): pl.pallas_call(functools.partial(compute_kernel, dims), grid=(samples //...  36.6 us
    pallas_call x1, Pallas kernels, gather(): pl.pallas_call(functools.partial(gather_kernel, (bands, peers, slices, li...  28.2 us

profile of v1, /device:TPU:1, one launch (start us, length us, event | category | flops | bytes accessed | tf_op | source)
XLA Modules:
  0.0 64.9 jit_solution(15593043726817599713)
XLA Ops:
  0.0 28.2 %gather_filters.1 = (f32[8,40,128]{2,1,0:T(8,128)}, f32[8,40,1024]{2,1,0:T(8,128)}, f32[8,40,1024]{2,1,0:T(8,128)}, f32[6,1,128]{2,1,0:T(1,128)}, f32[6,8,128]{2,1,0:T(8,128)}, /*index=5*/f32[8,128]{1,0:T(8,128)}) custom-call(f32[40,128]{1,0:T(8,128)} %low_ref.1, f32[40,1024]{1,0:T(8,128)} %mid_ref.1, f32[40,1024]{1,0:T(8,128)} %high_ref.1, ...), custom_call_target="tpu_custom_call" | custom-call | tf_op jit(solution)/shard_map/gather_filters/pallas_call | solution.py:188
  28.2 36.6 %filter_templates.1 = f32[1,256,8192]{2,1,0:T(8,128)} custom-call(s32[3]{0:T(128)} %count_ref.1, f32[320,128]{1,0:T(8,128)} %bitcast.9, f32[320,1024]{1,0:T(8,128)} %bitcast.7, f32[320,1024]{1,0:T(8,128)} %bitcast.8, f32[6,1,128]{2,1,0:T(1,128)} %get-tuple-element.14.x_low, f32[48,128]{1,0:T(8,128)} %bitcast.12, f32[8,128]{1,0:T(8,128)} %get-tuple-element.16.x_prev, ...), custom_call_target="tpu_custom_call" | custom-call | tf_op jit(solution)/shard_map/filter_templates/pallas_call | solution.py:335

commit v2 on v1

v2 whole, which is shorter than its diff:
```python
import functools
import math

import jax
import jax.numpy as jnp
import numpy as np
from jax import lax
from jax.experimental import pallas as pl
from jax.experimental.pallas import tpu as pltpu
from jax.sharding import PartitionSpec as P

RATIO = 8
HALF_TAPS = 8
LANES = 128
WIDE = 256
MESH = pl.DeviceIdType.MESH


def upsample_matrix(rows, cols):
    u = np.arange(rows)[:, None]
    v = np.arange(cols)[None, :]
    lag = u - v // RATIO
    offset = (v % RATIO) / RATIO - (lag - HALF_TAPS)
    value = np.sinc(offset) * (0.5 + 0.5 * np.cos(np.pi * offset / (HALF_TAPS + 1)))
    return np.where((lag >= 0) & (lag < 2 * HALF_TAPS), value, 0.0).astype(np.float32)


def gather_kernel(
    sizes, count_ref, low_ref, mid_ref, high_ref, sl_ref, sm_ref, sh_ref, g_top, g_rest,
    recon_low, recon_mid, recon_high,
    w_top, w_rest, p_top, p_rest, frames_top, frames_rest,
    low_all, mid_all, high_all, sl_all, sm_all, sh_prev,
    low_r, mid_r, high_r, recon_sem, frame_sem, x_full,
    fl_top, fl_rest, fm_top, fm_rest, fh_top, fh_rest,
    strain_send, strain_recv, lz_send, lz_recv, lx_send, lx_recv,
    z_send, z_recv, x_send, x_recv, y_send, y_recv, d_send, d_recv, c_send, c_recv,
):
    bands, peers, slices, lines, parts = sizes
    rings = peers // lines
    b, p, y = lax.axis_index("band"), lax.axis_index("tmpl"), lax.axis_index("tm")
    z, x = p // lines, p % lines
    part = y % parts

    def along_z(k):
        return (b, ((z + k) % rings) * lines + x, y)

    def along_y(m):
        return (b, p, y - part + (part + m) % parts)

    across = (b, z * lines + (x + 1) % lines, y)
    sibling = (1 - b, p, y)
    barrier = pltpu.get_barrier_semaphore()
    others = [along_z(k) for k in range(1, rings)] + [sibling]
    others += [(b, p, (y + k) % slices) for k in range(1, slices)]
    if lines > 1:
        others += [across]
    for device in others:
        pl.semaphore_signal(barrier, inc=1, device_id=device, device_id_type=MESH)
    pl.semaphore_wait(barrier, len(others))

    sent, strains, landed = [], [], ([], [])

    def send(src, dst, sems, at, device):
        copy = pltpu.make_async_remote_copy(
            src_ref=src, dst_ref=dst, send_sem=sems[0].at[at], recv_sem=sems[1].at[at],
            device_id=device, device_id_type=MESH,
        )
        copy.start()
        sent.append(copy)
        return copy

    strain = (strain_send, strain_recv)
    for k in range(1, slices):
        device = (b, p, (y + k) % slices)
        strains.append(send(sl_ref, sl_all.at[2 + y], strain, (0, k), device))
        strains.append(send(sm_ref, sm_all.at[2 + y], strain, (1, k), device))
    if slices > 1:
        tail = sh_prev.shape[0]
        last = sh_ref.at[pl.ds(sh_ref.shape[0] - tail, tail)]
        strains.append(send(last, sh_prev, strain, (2, 1), (b, p, (y + 1) % slices)))

    arrays = ((mid_ref, mid_all), (high_ref, high_all))
    size = [ref.shape[1] // (bands * parts) for ref, _ in arrays]

    def cols(a, m=0):
        start = (b * parts + (part + m) % parts) * size[a]
        return pl.ds(pl.multiple_of(start, LANES), size[a])

    def shard(k, other=0):
        return ((z + rings - k) % rings) * lines + (x + other) % lines

    low_z = {k: send(low_ref, low_all.at[p], (lz_send, lz_recv), k, along_z(k)) for k in range(1, rings)}
    from_z, from_x, from_y, from_d = {}, {}, {}, {}
    low_x = {}
    if lines > 1:
        low_x[0] = send(low_ref, low_all.at[p], (lx_send, lx_recv), 0, across)
    for a, (ref, full) in enumerate(arrays):
        for k in range(1, rings):
            from_z[a, k] = send(
                ref.at[:, cols(a)], full.at[p, :, cols(a)], (z_send, z_recv), (a, k), along_z(k)
            )
        if lines > 1:
            for m in range(parts):
                piece = send(
                    ref.at[:, cols(a, m)], full.at[p, :, cols(a, m)],
                    (x_send, x_recv) if m == 0 else (d_send, d_recv), (a, m, 0), across,
                )
                (from_x if m == 0 else from_d)[a, m, 0] = piece
    low_all[p] = low_ref[...]
    mid_all[p] = mid_ref[...]
    high_all[p] = high_ref[...]
    for ref, value in ((sl_all, sl_ref), (sm_all, sm_ref)):
        zero = jnp.zeros(value.shape, jnp.float32)
        ref[0] = zero
        ref[1] = zero
        ref[slices + 2] = zero
        ref[slices + 3] = zero
        ref[2 + y] = value[...]
    if slices == 1:
        sh_prev[...] = jnp.zeros(sh_prev.shape, jnp.float32)

    count = [0]

    def pass_on(a, view):
        at = (a, count[0])
        count[0] += 1
        landed[a].append(send(view, view, (c_send, c_recv), at, sibling))

    recons = []
    for i, (src, dst) in enumerate(((recon_low, low_r), (recon_mid, mid_r), (recon_high, high_r))):
        copy = pltpu.make_async_copy(src.at[:, b, :], dst, recon_sem.at[i])
        copy.start()
        recons.append(copy)
    for copy in strains:
        copy.wait_recv()
    before = sh_prev.shape[0]
    x_full[:before] = jnp.where(y > 0, sh_prev[...], 0.0)
    x_full[before:] = sh_ref[...]
    chunks = fh_top.shape[0] // LANES - 1
    stride = -(-chunks // 3)
    stores = []

    def frames_part(i):
        first, last = i * stride, min(chunks, (i + 1) * stride)
        fill_frames(lambda r: x_full[pl.ds(r, 1), :], fh_top, fh_rest, chunks, first, last)
        low, high = (chunks + 1 - last) * LANES if last < chunks else 0, (chunks + 1 - first) * LANES
        for j, (src, dst) in enumerate(((fh_top, frames_top), (fh_rest, frames_rest))):
            rows = pl.ds(low, high - low)
            copy = pltpu.make_async_copy(src.at[rows], dst.at[rows], frame_sem.at[i, j])
            copy.start()
            stores.append(copy)

    frames_part(0)
    for k in range(1, rings):
        low_z[k].wait_recv()
        if lines > 1:
            view = low_all.at[shard(k)]
            low_x[k] = send(view, view, (lx_send, lx_recv), k, across)
    for a, (_, full) in enumerate(arrays):
        count[0] = 0
        for k in range(1, rings):
            from_z[a, k].wait_recv()
            view = full.at[shard(k), :, cols(a)]
            if lines > 1:
                from_x[a, 0, k] = send(view, view, (x_send, x_recv), (a, 0, k), across)
            for m in range(1, parts):
                from_y[a, m, k] = send(view, view, (y_send, y_recv), (a, m, k), along_y(m))
            pass_on(a, view)
    base = count[0]
    frames_part(1)
    for a, (_, full) in enumerate(arrays):
        count[0] = base
        for k in range(rings):
            if lines > 1:
                from_x[a, 0, k].wait_recv()
                view = full.at[shard(k, 1), :, cols(a)]
                if k > 0:
                    for m in range(1, parts):
                        from_d[a, m, k] = send(view, view, (d_send, d_recv), (a, m, k), along_y(m))
                pass_on(a, view)
            for m in range(1, parts):
                if k == 0:
                    continue
                from_y[a, m, k].wait_recv()
                view = full.at[shard(k), :, cols(a, parts - m)]
                pass_on(a, view)
    base = count[0]
    frames_part(2)

    def last_pieces(a, full):
        count[0] = base
        for k in range(rings):
            for m in range(1, parts):
                if lines > 1:
                    from_d[a, m, k].wait_recv()
                    shift = m if k == 0 else parts - m
                    pass_on(a, full.at[shard(k, 1), :, cols(a, shift)])

    low_here, mid_here, low_total, mid_total = bounds(sl_ref, sm_ref, slices)
    taps_low, taps_mid = low_ref.shape[1], mid_ref.shape[1]
    low_chunks, mid_chunks = (r.shape[0] // LANES - 1 for r in (fl_top, fm_top))
    rows_mid = mid_here // LANES

    def low_row(r):
        return sl_all[y + 1 - taps_low // LANES + r]

    def mid_row(r):
        at = r + (y + 2) * rows_mid - taps_mid // LANES - 1
        return sm_all[at // rows_mid, pl.ds(at % rows_mid, 1), :]

    fill_frames(shifted(low_row, HALF_TAPS + 1), fl_top, fl_rest, low_chunks)
    fill_frames(shifted(mid_row, HALF_TAPS), fm_top, fm_rest, mid_chunks)
    for copy in recons:
        copy.wait()
    last_pieces(*(0, mid_all))
    for copy in low_x.values():
        copy.wait_recv()
    low_w = split(template_filters(low_r, low_all, count_ref[2]))
    parts_low = []
    for c in range(low_chunks):
        at = (low_chunks - 1 - c) * LANES
        parts_low.append(dot3(low_w, (fl_top[at : at + LANES, :LANES], fl_rest[at : at + LANES, :LANES])))
    low = jnp.concatenate(parts_low, axis=1)
    time = y * low_here - (HALF_TAPS + 1) + lax.broadcasted_iota(jnp.int32, low.shape, 1)
    low = split(jnp.where((time >= 0) & (time < low_total), low, 0.0))
    for copy in landed[0]:
        copy.wait_recv()
    mid_w = split(template_filters(mid_r, mid_all, count_ref[1]))
    last_pieces(*(1, high_all))
    width, columns = g_top.shape[1], p_top.shape[1]
    for start in range(0, columns, WIDE):
        size_here = min(WIDE, columns - start)
        at = (mid_chunks - taps_mid // LANES - start // LANES) * LANES
        frames = (fm_top[at : at + taps_mid, :size_here], fm_rest[at : at + taps_mid, :size_here])
        value = dot3(mid_w, frames)
        base_col, lead = start // width * LANES, start % width
        tile = slice(lead, lead + size_here)
        pieces = tuple(v[:, base_col : base_col + WIDE] for v in low)
        value += dot3(pieces, (g_top[:, tile], g_rest[:, tile]))
        time = y * mid_here - HALF_TAPS + start + lax.broadcasted_iota(jnp.int32, value.shape, 1)
        top, rest = split(jnp.where((time >= 0) & (time < mid_total), value, 0.0))
        p_top[:, start : start + size_here] = top
        p_rest[:, start : start + size_here] = rest
    for copy in landed[1]:
        copy.wait_recv()
    w_top[...], w_rest[...] = split(template_filters(high_r, high_all, count_ref[0]))
    for copy in sent:
        copy.wait_send()
    for copy in stores:
        copy.wait()


def bounds(s_low, s_mid, slices):
    low, mid = s_low.shape[0] * LANES, s_mid.shape[0] * LANES
    return low, mid, low * slices, mid * slices


def template_filters(recon_ref, full, count):
    peers, rows, taps = full.shape
    first = (((0,), (0,)), ((), ()))
    index = lax.broadcasted_iota(jnp.int32, recon_ref.shape, 0)
    recon = jnp.where(index < count, recon_ref[...], 0.0)
    if rows % 8 == 0:
        return dot3(split(recon), split(full[...].reshape(peers * rows, taps)), first)
    total = 0.0
    for p in range(peers):
        total += dot3(split(recon[p * rows : (p + 1) * rows]), split(full[p]), first)
    return total


def gather(sizes, count, filters, strains, g, recons):
    low, mid, high = filters
    s_low, s_mid, s_high = strains
    bands, peers, slices = sizes
    lines = 2 if peers % 2 == 0 else 1
    rings = peers // lines
    parts = math.gcd(slices, min(mid.shape[1], high.shape[1]) // (bands * LANES))
    f32, half = jnp.float32, jnp.bfloat16
    basis, _, tmpl = recons[0].shape
    taps_low, taps_mid, taps = (f.shape[1] for f in filters)
    low_here, mid_here, _, _ = bounds(s_low, s_mid, slices)
    samples = s_high.shape[0] * LANES
    columns = mid_here + LANES
    vmem = pl.BlockSpec(memory_space=pltpu.VMEM)
    anywhere = pl.BlockSpec(memory_space=pl.ANY)
    dma = pltpu.SemaphoreType.DMA

    def two(*dims):
        return [dma(dims)] * 2

    def frames(rows):
        return [pltpu.VMEM((rows, WIDE), half)] * 2

    return pl.pallas_call(
        functools.partial(gather_kernel, (bands, peers, slices, lines, parts)),
        out_shape=[jax.ShapeDtypeStruct((tmpl, taps), half)] * 2
        + [jax.ShapeDtypeStruct((tmpl, columns), half)] * 2
        + [jax.ShapeDtypeStruct((samples + taps, WIDE), half)] * 2,
        in_specs=[pl.BlockSpec(memory_space=pltpu.SMEM)] + [vmem] * 8 + [anywhere] * 3,
        out_specs=[vmem] * 4 + [anywhere] * 2,
        scratch_shapes=[pltpu.VMEM((peers,) + a.shape, f32) for a in filters]
        + [pltpu.VMEM((slices + 4,) + a.shape, f32) for a in (s_low, s_mid)]
        + [pltpu.VMEM((taps // LANES, LANES), f32)]
        + [pltpu.VMEM((basis, tmpl), f32)] * 3
        + [dma((3,)), dma((3, 2)), pltpu.VMEM(((samples + taps) // LANES, LANES), f32)]
        + frames(low_here + 2 * LANES + taps_low) + frames(columns + taps_mid) + frames(samples + taps)
        + two(3, slices) + two(rings) + two(rings) + two(2, rings)
        + two(2, parts, rings) * 3 + two(2, peers * parts),
        compiler_params=pltpu.CompilerParams(
            collective_id=0, has_side_effects=True, vmem_limit_bytes=60 * 1024 * 1024
        ),
        name="gather_filters",
    )(count, *filters, *strains, *g, *recons)


def split(value):
    top = value.astype(jnp.bfloat16)
    return top, (value - top.astype(jnp.float32)).astype(jnp.bfloat16)


def dot3(a, b, dims=(((1,), (0,)), ((), ()))):
    def one(u, v):
        return lax.dot_general(u, v, dims, preferred_element_type=jnp.float32)

    return one(a[0], b[0]) + one(a[0], b[1]) + one(a[1], b[0])


def staggered(row):
    return pltpu.roll(jnp.broadcast_to(row, (LANES, LANES)), 0, 1, stride=1, stride_axis=0)


def shifted(read, by):
    lane = lax.broadcasted_iota(jnp.int32, (1, LANES), 1)

    def row(r):
        late = [pltpu.roll(read(r + i), by, 1) for i in range(2)]
        return jnp.where(lane >= by, late[1], late[0])

    return row


def fill_frames(row, top_ref, rest_ref, chunks, first=0, last=None):
    lane = lax.broadcasted_iota(jnp.int32, (LANES, LANES), 1)
    lag = lax.broadcasted_iota(jnp.int32, (LANES, LANES), 0)

    def step(c, before):
        now = staggered(row(c + 1))
        top, rest = split(jnp.where(lane >= lag, now, before))
        left = pl.multiple_of((chunks - 1 - c) * LANES, LANES)
        right = pl.multiple_of((chunks - c) * LANES, LANES)
        for ref, value in ((top_ref, top), (rest_ref, rest)):
            ref[pl.ds(left, LANES), :LANES] = value
            ref[pl.ds(right, LANES), LANES:] = value
        return now

    lax.fori_loop(first, chunks if last is None else last, step, staggered(row(first)))


def compute_kernel(
    w_top, w_rest, p_top, p_rest, g_top, g_rest, frames_top, frames_rest,
    out_ref, fh_top, fh_rest, frame_sem,
):
    step = pl.program_id(0)
    blocks = pl.num_programs(0)
    taps = w_top.shape[1]
    width = out_ref.shape[2]
    chunks = fh_top.shape[0] // LANES - 1

    def block(j):
        rows = pl.ds(pl.multiple_of(j * width, width), width)
        return [
            pltpu.make_async_copy(src.at[rows], dst.at[rows], frame_sem.at[j, i])
            for i, (src, dst) in enumerate(((frames_top, fh_top), (frames_rest, fh_rest)))
        ]

    total = fh_top.shape[0] // width
    ahead = taps // width

    @pl.when(step == 0)
    def _():
        for j in reversed(range(total)):
            for copy in block(j):
                copy.start()
        for j in range(total - ahead, total):
            for copy in block(j):
                copy.wait()

    for copy in block(blocks - 1 - step):
        copy.wait()
    base = pl.multiple_of(step * (width // RATIO), LANES)
    pieces = (p_top[:, pl.ds(base, WIDE)], p_rest[:, pl.ds(base, WIDE)])
    for start in range(0, width, WIDE):
        at = (chunks - taps // LANES - start // LANES - step * (width // LANES)) * LANES
        rows = pl.ds(pl.multiple_of(at, LANES), taps)
        value = dot3((w_top[...], w_rest[...]), (fh_top[rows, :], fh_rest[rows, :]))
        tile = slice(start, start + WIDE)
        out_ref[0, :, tile] = value + dot3(pieces, (g_top[:, tile], g_rest[:, tile]))


def compute(w, p, g, frames):
    tmpl, taps = w[0].shape
    rows = frames[0].shape[0]
    samples = rows - taps
    width = g[0].shape[1]
    vmem = pl.BlockSpec(memory_space=pltpu.VMEM)
    return pl.pallas_call(
        compute_kernel,
        grid=(samples // width,),
        out_shape=jax.ShapeDtypeStruct((1, tmpl, samples), jnp.float32),
        in_specs=[vmem] * 6 + [pl.BlockSpec(memory_space=pl.ANY)] * 2,
        out_specs=pl.BlockSpec((1, tmpl, width), lambda i: (0, 0, i)),
        scratch_shapes=[pltpu.VMEM((rows, WIDE), jnp.bfloat16)] * 2
        + [pltpu.SemaphoreType.DMA((rows // width, 2))],
        compiler_params=pltpu.CompilerParams(vmem_limit_bytes=60 * 1024 * 1024),
        name="filter_templates",
    )(*w, *p, *g, *frames)


def local(
    sizes, strain_high, strain_mid, strain_low, filters_high, filters_mid, filters_low,
    recon_high, recon_mid, recon_low, basis_count,
):
    matrix = upsample_matrix(WIDE, RATIO * LANES)
    top = matrix.astype(jnp.bfloat16)
    rest = (matrix - top.astype(np.float32)).astype(jnp.bfloat16)
    g = (jnp.asarray(top), jnp.asarray(rest))
    strains = [s.reshape(-1, LANES) for s in (strain_low, strain_mid, strain_high)]
    out = gather(
        sizes, basis_count, (filters_low, filters_mid, filters_high), strains, g,
        (recon_low, recon_mid, recon_high),
    )
    return compute(out[:2], out[2:4], g, out[4:])


def solution(mesh):
    sizes = tuple(mesh.shape[name] for name in ("band", "tmpl", "tm"))
    in_specs = (
        P("tm"), P("tm"), P("tm"),
        P("tmpl", None), P("tmpl", None), P("tmpl", None),
        P(None, None, "tmpl"), P(None, None, "tmpl"), P(None, None, "tmpl"),
        P(),
    )
    return jax.shard_map(
        functools.partial(local, sizes), mesh=mesh, in_specs=in_specs,
        out_specs=P("band", "tmpl", "tm"), check_vma=False,
    )
```

time: 65 us -> 58.5 us (0.900)
  Pallas kernels: 64.8 us -> 58.3 us
    pallas_call x1, Pallas kernels: 36.6 us -> 22.5 us  [compute(): pl.pallas_call(compute_kernel, grid=(samples // width,), out_shape=jax.Sh...]
    pallas_call x1, Pallas kernels: 28.2 us -> 35.8 us  [gather(): pl.pallas_call(functools.partial(gather_kernel, (bands, peers, slices, li...]
where the time goes in v2:
time: 58.5 us; the launch traced here: 58.3 us
  Pallas kernels  58.3 us (100%)
    pallas_call x1, Pallas kernels, gather(): pl.pallas_call(functools.partial(gather_kernel, (bands, peers, slices, li...  35.8 us
    pallas_call x1, Pallas kernels, compute(): pl.pallas_call(compute_kernel, grid=(samples // width,), out_shape=jax.Sh...  22.5 us

profile of v2, /device:TPU:1, one launch (start us, length us, event | category | flops | bytes accessed | tf_op | source)
XLA Modules:
  0.0 58.3 jit_solution(16769461485872848974)
XLA Ops:
  0.0 35.8 %gather_filters.1 = (bf16[256,1024]{1,0:T(8,128)(2,1)}, bf16[256,1024]{1,0:T(8,128)(2,1)}, bf16[256,1152]{1,0:T(8,128)(2,1)}, bf16[256,1152]{1,0:T(8,128)(2,1)},...) custom-call(s32[3]{0:T(128)} %count_ref.1, f32[40,128]{1,0:T(8,128)} %low_ref.1, f32[40,1024]{1,0:T(8,128)} %mid_ref.1, ...), custom_call_target="tpu_custom_call" | custom-call | tf_op jit(solution)/shard_map/gather_filters/pallas_call | solution.py:294
  35.8 22.5 %filter_templates.1 = f32[1,256,8192]{2,1,0:T(8,128)} custom-call(bf16[256,1024]{1,0:T(8,128)(2,1)} %get-tuple-element.11.w_top, bf16[256,1024]{1,0:T(8,128)(2,1)} %get-tuple-element.12.w_rest, bf16[256,1152]{1,0:T(8,128)(2,1)} %get-tuple-element.13.p_top, bf16[256,1152]{1,0:T(8,128)(2,1)} %get-tuple-element.14.p_rest, ...), custom_call_target="tpu_custom_call" | custom-call | tf_op jit(solution)/shard_map/filter_templates/pallas_call | solution.py:406

commit v3 on v2

--- a/solution.py
+++ b/solution.py
@@ -137,7 +137,7 @@
     x_full[:before] = jnp.where(y > 0, sh_prev[...], 0.0)
     x_full[before:] = sh_ref[...]
     chunks = fh_top.shape[0] // LANES - 1
-    stride = -(-chunks // 3)
+    stride = -(-chunks // 6)
     stores = []
 
     def frames_part(i):
@@ -166,8 +166,8 @@
             for m in range(1, parts):
                 from_y[a, m, k] = send(view, view, (y_send, y_recv), (a, m, k), along_y(m))
             pass_on(a, view)
+        frames_part(1 + a)
     base = count[0]
-    frames_part(1)
     for a, (_, full) in enumerate(arrays):
         count[0] = base
         for k in range(rings):
@@ -184,8 +184,9 @@
                 from_y[a, m, k].wait_recv()
                 view = full.at[shard(k), :, cols(a, parts - m)]
                 pass_on(a, view)
+        frames_part(3 + a)
     base = count[0]
-    frames_part(2)
+    frames_part(5)
 
     def last_pieces(a, full):
         count[0] = base
@@ -302,7 +303,7 @@
         + [pltpu.VMEM((slices + 4,) + a.shape, f32) for a in (s_low, s_mid)]
         + [pltpu.VMEM((taps // LANES, LANES), f32)]
         + [pltpu.VMEM((basis, tmpl), f32)] * 3
-        + [dma((3,)), dma((3, 2)), pltpu.VMEM(((samples + taps) // LANES, LANES), f32)]
+        + [dma((3,)), dma((6, 2)), pltpu.VMEM(((samples + taps) // LANES, LANES), f32)]
         + frames(low_here + 2 * LANES + taps_low) + frames(columns + taps_mid) + frames(samples + taps)
         + two(3, slices) + two(rings) + two(rings) + two(2, rings)
         + two(2, parts, rings) * 3 + two(2, peers * parts),
@@ -389,12 +390,22 @@
         copy.wait()
     base = pl.multiple_of(step * (width // RATIO), LANES)
     pieces = (p_top[:, pl.ds(base, WIDE)], p_rest[:, pl.ds(base, WIDE)])
+    near = [piece[:, :LANES] for piece in pieces]
+    stacked = jnp.concatenate(near, axis=1)
     for start in range(0, width, WIDE):
         at = (chunks - taps // LANES - start // LANES - step * (width // LANES)) * LANES
         rows = pl.ds(pl.multiple_of(at, LANES), taps)
         value = dot3((w_top[...], w_rest[...]), (fh_top[rows, :], fh_rest[rows, :]))
         tile = slice(start, start + WIDE)
-        out_ref[0, :, tile] = value + dot3(pieces, (g_top[:, tile], g_rest[:, tile]))
+        if (start + WIDE) // RATIO + 2 * HALF_TAPS <= LANES:
+            top = g_top[:LANES, tile]
+            value += jnp.dot(
+                stacked, jnp.concatenate([top, top], axis=0), preferred_element_type=jnp.float32
+            )
+            value += jnp.dot(near[0], g_rest[:LANES, tile], preferred_element_type=jnp.float32)
+        else:
+            value += dot3(pieces, (g_top[:, tile], g_rest[:, tile]))
+        out_ref[0, :, tile] = value
 
 
 def compute(w, p, g, frames):

time: 58.5 us -> 58.5 us (level)
    pallas_call x1, Pallas kernels: 35.8 us -> 36.6 us  [gather(): pl.pallas_call(functools.partial(gather_kernel, (bands, peers, slices, li...]
    pallas_call x1, Pallas kernels: 22.5 us -> 21.7 us  [compute(): pl.pallas_call(compute_kernel, grid=(samples // width,), out_shape=jax.Sh...]
where the time goes in v3:
time: 58.5 us; the launch traced here: 58.4 us
  Pallas kernels  58.3 us (100%)
    pallas_call x1, Pallas kernels, gather(): pl.pallas_call(functools.partial(gather_kernel, (bands, peers, slices, li...  36.6 us
    pallas_call x1, Pallas kernels, compute(): pl.pallas_call(compute_kernel, grid=(samples // width,), out_shape=jax.Sh...  21.7 us

profile of v3, /device:TPU:1, one launch (start us, length us, event | category | flops | bytes accessed | tf_op | source)
XLA Modules:
  0.0 58.4 jit_solution(963233175708518305)
XLA Ops:
  0.0 36.6 %gather_filters.1 = (bf16[256,1024]{1,0:T(8,128)(2,1)}, bf16[256,1024]{1,0:T(8,128)(2,1)}, bf16[256,1152]{1,0:T(8,128)(2,1)}, bf16[256,1152]{1,0:T(8,128)(2,1)},...) custom-call(s32[3]{0:T(128)} %count_ref.1, f32[40,128]{1,0:T(8,128)} %low_ref.1, f32[40,1024]{1,0:T(8,128)} %mid_ref.1, ...), custom_call_target="tpu_custom_call" | custom-call | tf_op jit(solution)/shard_map/gather_filters/pallas_call | solution.py:295
  36.6 21.7 %filter_templates.1 = f32[1,256,8192]{2,1,0:T(8,128)} custom-call(bf16[256,1024]{1,0:T(8,128)(2,1)} %get-tuple-element.11.w_top, bf16[256,1024]{1,0:T(8,128)(2,1)} %get-tuple-element.12.w_rest, bf16[256,1152]{1,0:T(8,128)(2,1)} %get-tuple-element.13.p_top, bf16[256,1152]{1,0:T(8,128)(2,1)} %get-tuple-element.14.p_rest, ...), custom_call_target="tpu_custom_call" | custom-call | tf_op jit(solution)/shard_map/filter_templates/pallas_call | solution.py:417

commit v4 on v3

--- a/solution.py
+++ b/solution.py
@@ -137,7 +137,7 @@
     x_full[:before] = jnp.where(y > 0, sh_prev[...], 0.0)
     x_full[before:] = sh_ref[...]
     chunks = fh_top.shape[0] // LANES - 1
-    stride = -(-chunks // 6)
+    stride = -(-chunks // 3)
     stores = []
 
     def frames_part(i):
@@ -166,7 +166,6 @@
             for m in range(1, parts):
                 from_y[a, m, k] = send(view, view, (y_send, y_recv), (a, m, k), along_y(m))
             pass_on(a, view)
-        frames_part(1 + a)
     base = count[0]
     for a, (_, full) in enumerate(arrays):
         count[0] = base
@@ -184,9 +183,9 @@
                 from_y[a, m, k].wait_recv()
                 view = full.at[shard(k), :, cols(a, parts - m)]
                 pass_on(a, view)
-        frames_part(3 + a)
     base = count[0]
-    frames_part(5)
+    frames_part(1)
+    frames_part(2)
 
     def last_pieces(a, full):
         count[0] = base
@@ -303,7 +302,7 @@
         + [pltpu.VMEM((slices + 4,) + a.shape, f32) for a in (s_low, s_mid)]
         + [pltpu.VMEM((taps // LANES, LANES), f32)]
         + [pltpu.VMEM((basis, tmpl), f32)] * 3
-        + [dma((3,)), dma((6, 2)), pltpu.VMEM(((samples + taps) // LANES, LANES), f32)]
+        + [dma((3,)), dma((3, 2)), pltpu.VMEM(((samples + taps) // LANES, LANES), f32)]
         + frames(low_here + 2 * LANES + taps_low) + frames(columns + taps_mid) + frames(samples + taps)
         + two(3, slices) + two(rings) + two(rings) + two(2, rings)
         + two(2, parts, rings) * 3 + two(2, peers * parts),

time: 58.5 us -> 60.9 us (1.041)
  Pallas kernels: 58.3 us -> 60.7 us
    pallas_call x1, Pallas kernels: 36.6 us -> 38.9 us  [gather(): pl.pallas_call(functools.partial(gather_kernel, (bands, peers, slices, li...]
where the time goes in v4:
time: 60.9 us; the launch traced here: 60.7 us
  Pallas kernels  60.7 us (100%)
    pallas_call x1, Pallas kernels, gather(): pl.pallas_call(functools.partial(gather_kernel, (bands, peers, slices, li...  38.9 us
    pallas_call x1, Pallas kernels, compute(): pl.pallas_call(compute_kernel, grid=(samples // width,), out_shape=jax.Sh...  21.7 us

profile of v4, /device:TPU:1, one launch (start us, length us, event | category | flops | bytes accessed | tf_op | source)
XLA Modules:
  0.0 60.7 jit_solution(16173684947008064536)
XLA Ops:
  0.0 38.9 %gather_filters.1 = (bf16[256,1024]{1,0:T(8,128)(2,1)}, bf16[256,1024]{1,0:T(8,128)(2,1)}, bf16[256,1152]{1,0:T(8,128)(2,1)}, bf16[256,1152]{1,0:T(8,128)(2,1)},...) custom-call(s32[3]{0:T(128)} %count_ref.1, f32[40,128]{1,0:T(8,128)} %low_ref.1, f32[40,1024]{1,0:T(8,128)} %mid_ref.1, ...), custom_call_target="tpu_custom_call" | custom-call | tf_op jit(solution)/shard_map/gather_filters/pallas_call | solution.py:294
  38.9 21.7 %filter_templates.1 = f32[1,256,8192]{2,1,0:T(8,128)} custom-call(bf16[256,1024]{1,0:T(8,128)(2,1)} %get-tuple-element.11.w_top, bf16[256,1024]{1,0:T(8,128)(2,1)} %get-tuple-element.12.w_rest, bf16[256,1152]{1,0:T(8,128)(2,1)} %get-tuple-element.13.p_top, bf16[256,1152]{1,0:T(8,128)(2,1)} %get-tuple-element.14.p_rest, ...), custom_call_target="tpu_custom_call" | custom-call | tf_op jit(solution)/shard_map/filter_templates/pallas_call | solution.py:416
